TPU v7x, 32 devices: a whole 2x2x4 slice. The times are simulated.
32 devices in a mesh: row: 4 (over x, core), col: 8 (over z, y).
Axes of the slice: x: 2, y: 2, z: 4, core: 2. Of those that a mesh axis runs over, the one named last changes fastest.
Arguments:
- momentum: bfloat16 [8704, 30720], P('row', 'col'), may hold values from -6 to 6
- grad: bfloat16 [8704, 30720], P('row', 'col'), may hold values from -6 to 6
- q_prev: bfloat16 [30720, 512], P('col'), may hold values from -6 to 6
- row_counts: int32 [4], replicated, may hold values from 1 to 17, 64 in all
- col_counts: int32 [8], replicated, may hold values from 1 to 30, 224 in all
Outputs:
- momentum_out: bfloat16 [8704, 30720], P('row', 'col')
- basis_out: bfloat16 [30720, 512], P('col')
- update: bfloat16 [8704, 30720], P('row', 'col')
Inputs may be any that keep to these rules, and one draw needn't show every extreme that they name: `row_counts`: each index of row holds 1 to 17 live row blocks, the counts sum to 64, and some index holds exactly 17; live blocks are the first slots of a device. `col_counts`: each index of col holds 1 to 30 live column blocks, the counts sum to 224, and some index holds exactly 30; live blocks are the first slots of a device.
All inputs are finite; a program needn't handle non-finite values.
Results may differ from a plain program's by a relative error of at most 0.0079.
Values may be sent and summed in bfloat16 or wider, within the bound.
No kernel may reach another device: no remote copies, remote signals or barrier semaphores. Data moves between devices by JAX's collectives and lax.ppermute only.
A program may use at most 128 MiB of HBM per device.

v0:
```python
import math
import jax
import jax.numpy as jnp
from jax import lax
from jax.sharding import PartitionSpec as P

D = 8192
FF = 28672
RANK = 512
BLOCK = 128
EPS = 1e-06
ERR = 0.05


def tri_inverse(gram_matrix):
    lower_factor = jnp.linalg.cholesky(gram_matrix)
    ident = jnp.eye(gram_matrix.shape[0], dtype=gram_matrix.dtype)
    return jax.scipy.linalg.solve_triangular(lower_factor, ident, lower=True)


def on_device(momentum, grad, q_prev, row_counts, col_counts):
    row_slots, col_slots = momentum.shape
    row_live = row_counts[lax.axis_index("row")] * BLOCK
    col_live = col_counts[lax.axis_index("col")] * BLOCK
    row_mask = jnp.arange(row_slots, dtype=jnp.int32) < row_live
    col_mask = jnp.arange(col_slots, dtype=jnp.int32) < col_live
    summed = (momentum.astype(jnp.float32) + grad.astype(jnp.float32)).astype(jnp.bfloat16)
    buffer = jnp.where(row_mask[:, None] & col_mask[None, :], summed, jnp.zeros((), jnp.bfloat16))
    prev_basis = jnp.where(col_mask[:, None], q_prev, jnp.zeros((), jnp.bfloat16))
    partial_left = jnp.dot(buffer, prev_basis, preferred_element_type=jnp.float32)
    left_part = lax.psum(partial_left, "col")
    gram_local = jnp.dot(left_part.T, left_part, precision=lax.Precision.HIGHEST)
    gram_matrix = lax.psum(gram_local, "row")
    inverse = tri_inverse(gram_matrix)
    ortho = jnp.dot(left_part, inverse.T, precision=lax.Precision.HIGHEST).astype(jnp.bfloat16)
    right_part = lax.psum_scatter(
        lax.dot_general(
            buffer, ortho, (((0,), (0,)), ((), ())), preferred_element_type=jnp.float32
        ),
        "row",
        scatter_dimension=0,
        tiled=True,
    )
    squares = lax.psum(jnp.sum(right_part * right_part, axis=0), ("row", "col"))
    norm_factor = lax.rsqrt(squares / FF + EPS)
    right_piece = right_part.astype(jnp.bfloat16)
    basis_piece = (right_part * norm_factor[None, :]).astype(jnp.bfloat16)
    right_b, basis_out = (
        lax.all_gather(right_piece, "row", axis=0, tiled=True),
        lax.all_gather(basis_piece, "row", axis=0, tiled=True),
    )
    feedback = lax.dot_general(
        ortho, right_b, (((1,), (1,)), ((), ())), preferred_element_type=jnp.float32
    )
    momentum_out = (buffer.astype(jnp.float32) - ERR * feedback).astype(jnp.bfloat16)
    direction = lax.dot_general(
        ortho, basis_out, (((1,), (1,)), ((), ())), preferred_element_type=jnp.float32
    )
    update = (math.sqrt(D / RANK) * direction).astype(jnp.bfloat16)
    return (momentum_out, basis_out, update)


def solution(mesh):
    placed = (P("row", "col"), P("row", "col"), P("col", None), P(), P())
    return jax.shard_map(
        on_device,
        mesh=mesh,
        in_specs=placed,
        out_specs=(P("row", "col"), P("col", None), P("row", "col")),
        check_vma=False,
    )
```

profile of v0, /device:TPU:0, one launch (start us, length us, event | category | flops | bytes accessed | tf_op | source)
XLA Modules:
  0.0 635.1 jit_solution(6499399184790909212)
XLA Ops:
  11.0 15.4 %and_select_fusion = bf16[2176,3840]{1,0:T(8,128)(2,1)S(1)} fusion(bf16[2176,3840]{1,0:T(8,128)(2,1)} %param.6, bf16[2176,3840]{1,0:T(8,128)(2,1)} %param.5, pred[3840]{0:T(1024)(128)(4,1)S(1)} %iota_compare_fusion.4, pred[2176]{0:T(1024)(128)(4,1)S(1)} %iota_compare_fusion.5), kind=kLoop, calls=%fused_computation.5 | loop fusion | flops 50135040 | bytes 50141056 | tf_op jit(solution)/shard_map/jit(_where)/select_n | solution.py:28
  26.5 6.1 copy-done
  32.6 11.3 %fusion = f32[2176,512]{1,0:T(8,128)} fusion(bf16[2176,3840]{1,0:T(8,128)(2,1)S(1)} %and_select_fusion, bf16[3840,512]{1,0:T(8,128)(2,1)S(1)} %copy-done.1, pred[3840]{0:T(1024)(128)(4,1)S(1)} %iota_compare_fusion.4), kind=kOutput, calls=%fused_computation.7 | convolution fusion | flops 8558346240 | bytes 25104128 | tf_op jit(solution)/shard_map/dot_general | solution.py:30
  44.0 165.8 %all-reduce.4.cloned.1.call-done = f32[2176,512]{1,0:T(8,128)} async-done(((f32[2176,512]{1,0:T(8,128)}), f32[2176,512]{1,0:T(8,128)}) %all-reduce.4.cloned.1.call-update) | async-done | bytes 4456464 | tf_op jit(solution)/shard_map/psum | solution.py:31
  209.9 12.1 %fusion.45 = f32[512,512]{0,1:T(8,128)} fusion(f32[2176,512]{1,0:T(8,128)} %all-reduce.4.cloned.1.call-done), kind=kOutput, calls=%fused_computation.91 | convolution fusion | flops 6845104128 | bytes 5505024 | tf_op jit(solution)/shard_map/dot_general | solution.py:32
  223.1 34.3 %all-reduce.6.cloned.1.call-done = f32[512,512]{0,1:T(8,128)} async-done(((f32[512,512]{0,1:T(8,128)}), f32[512,512]{0,1:T(8,128)}) %all-reduce.6.cloned.1.call-update) | async-done | bytes 1048592 | tf_op jit(solution)/shard_map/psum | solution.py:33
  260.5 11.7 %cholesky.104 = f32[128,128]{1,0:T(8,128)S(1)} custom-call(f32[128,128]{1,0:T(8,128)S(1)} %cholesky.266), custom_call_target="Cholesky" | custom-call | tf_op jit(solution)/shard_map/jit(cholesky)/cholesky | solution.py:16
  272.2 9.8 %custom-call.31 = f32[1,128,128]{1,2,0:T(8,128)S(1)} custom-call(f32[1,128,128]{2,1,0:T(8,128)S(1)} %get-tuple-element.32), custom_call_target="InvertDiagBlocksLowerTriangular" | custom-call | tf_op jit(solution)/shard_map/jit(cholesky)/cholesky | solution.py:16
  282.8 11.7 %cholesky.217 = f32[128,128]{1,0:T(8,128)S(1)} custom-call(f32[128,128]{1,0:T(8,128)S(1)} %cholesky.270), custom_call_target="Cholesky" | custom-call | tf_op jit(solution)/shard_map/jit(cholesky)/cholesky | solution.py:16
  294.6 10.0 %custom-call.32 = f32[1,128,128]{1,2,0:T(8,128)S(1)} custom-call(f32[1,128,128]{2,1,0:T(8,128)S(1)} %get-tuple-element.29), custom_call_target="InvertDiagBlocksLowerTriangular" | custom-call | tf_op jit(solution)/shard_map/jit(cholesky)/cholesky | solution.py:16
  305.3 11.7 %cholesky.238 = f32[128,128]{1,0:T(8,128)S(1)} custom-call(f32[128,128]{1,0:T(8,128)S(1)} %cholesky.275), custom_call_target="Cholesky" | custom-call | tf_op jit(solution)/shard_map/jit(cholesky)/cholesky | solution.py:16
  317.7 9.8 %custom-call.33 = f32[1,128,128]{1,2,0:T(8,128)S(1)} custom-call(f32[1,128,128]{2,1,0:T(8,128)S(1)} %get-tuple-element.26), custom_call_target="InvertDiagBlocksLowerTriangular" | custom-call | tf_op jit(solution)/shard_map/jit(cholesky)/cholesky | solution.py:16
  328.1 11.7 %cholesky.255 = f32[128,128]{1,0:T(8,128)S(1)} custom-call(f32[128,128]{1,0:T(8,128)S(1)} %convolution_subtract_fusion.5), custom_call_target="Cholesky" | custom-call | tf_op jit(solution)/shard_map/jit(cholesky)/cholesky | solution.py:16
  344.3 10.1 %while.1 = (s32[]{:T(128)}, f32[512,512]{1,0:T(8,128)S(1)}, s32[4,2]{0,1:T(2,128)S(1)}, f32[4,128,128]{2,1,0:T(8,128)}, s32[]{:T(128)}) while((s32[]{:T(128)}, f32[512,512]{1,0:T(8,128)S(1)}, s32[4,2]{0,1:T(2,128)S(1)}, f32[4,128,128]{2,1,0:T(8,128)}, s32[]{:T(128)}) %tuple.32), condition=%wide.while_cond, body=%wide.while_body.sunk | while | flops 2 | bytes 132205 | solution.py:18
  354.4 40.1 %custom-call.34 = f32[4,128,128]{1,2,0:T(8,128)S(1)} custom-call(f32[4,128,128]{2,1,0:T(8,128)} %get-tuple-element.10), custom_call_target="InvertDiagBlocksLowerTriangular" | custom-call | tf_op jit(solution)/shard_map/jit(_solve_triangular)/triangular_solve | solution.py:18
  398.4 9.0 %convolution_convert_fusion = bf16[2176,512]{1,0:T(8,128)(2,1)S(1)} fusion(f32[2176,512]{1,0:T(8,128)} %all-reduce.4.cloned.1.call-done, f32[128,512]{1,0:T(8,128)S(1)} %fusion.31, f32[128,512]{1,0:T(8,128)S(1)} %fusion.32, f32[128,512]{1,0:T(8,128)S(1)} %fusion.34, f32[128,512]{1,0:T(8,128)S(1)} %fusion.22), kind=kOutput, calls=%fused_computation.6 | convolution fusion | flops 6847004672 | bytes 7733248 | tf_op jit(solution)/shard_map/dot_general | solution.py:35
  407.4 15.1 %fusion.46 = f32[3840,512]{1,0:T(8,128)} fusion(bf16[2176,3840]{1,0:T(8,128)(2,1)} %copy-done, bf16[2176,512]{1,0:T(8,128)(2,1)S(1)} %convolution_convert_fusion), kind=kOutput, calls=%fused_computation.92 | convolution fusion | flops 8556380160 | bytes 26804224 | tf_op jit(solution)/shard_map/dot_general | solution.py:37
  422.6 70.1 %reduce-scatter.2.cloned.1.call-done = f32[960,512]{1,0:T(8,128)} async-done(((f32[3840,512]{1,0:T(8,128)}), f32[960,512]{1,0:T(8,128)}) %reduce-scatter.2.cloned.1.call-update) | async-done | bytes 1966096 | tf_op jit(solution)/shard_map/reduce_scatter | solution.py:36
  494.4 39.3 %psum.23 = f32[512]{0:T(512)S(1)} all-reduce(f32[512]{0:T(512)S(1)} %multiply_reduce_fusion), channel_id=1, replica_groups=mesh['row'=4,'col'=8] {'row','col'}, use_global_device_ids=true, to_apply=%region_12.13 | all-reduce | flops 512 | bytes 4096 | tf_op jit(solution)/shard_map/psum | solution.py:44
  538.1 33.3 %all-gather.5.cloned.1.call-done = bf16[3840,512]{1,0:T(8,128)(2,1)} async-done(((bf16[960,512]{1,0:T(8,128)(2,1)}), bf16[3840,512]{1,0:T(8,128)(2,1)}) %all-gather.5.cloned.1.call-update) | async-done | bytes 3932176 | tf_op jit(solution)/shard_map/all_gather | solution.py:50
  571.4 13.9 %multiply_convert_fusion = bf16[2176,3840]{1,0:T(8,128)(2,1)} fusion(bf16[2176,512]{1,0:T(8,128)(2,1)S(1)} %convolution_convert_fusion, bf16[3840,512]{1,0:T(8,128)(2,1)} %all-gather.5.cloned.1.call-done), kind=kOutput, calls=%fused_computation.2 | convolution fusion | flops 8573091840 | bytes 22872064 | tf_op jit(solution)/shard_map/dot_general | solution.py:56
  585.3 20.5 %all-gather.3.cloned.1.call-done = bf16[3840,512]{1,0:T(8,128)(2,1)} async-done(((bf16[960,512]{1,0:T(8,128)(2,1)}), bf16[3840,512]{1,0:T(8,128)(2,1)}) %all-gather.3.cloned.1.call-update) | async-done | bytes 3932176 | tf_op jit(solution)/shard_map/all_gather | solution.py:49
  605.8 18.3 %subtract_convert_fusion = bf16[2176,3840]{1,0:T(8,128)(2,1)} fusion(bf16[2176,3840]{1,0:T(8,128)(2,1)} %copy-done, bf16[2176,512]{1,0:T(8,128)(2,1)S(1)} %convolution_convert_fusion, bf16[3840,512]{1,0:T(8,128)(2,1)} %all-gather.3.cloned.1.call-done), kind=kOutput, calls=%fused_computation.3 | convolution fusion | flops 8589803520 | bytes 39583744 | tf_op jit(solution)/shard_map/dot_general | solution.py:52
  624.1 4.3 copy.30
  (64 shorter events, 31.5 us)
Async XLA Ops:
  7.2 202.7 %all-reduce.4.cloned.1.call-start = ((), (), s32[]{:S(2)}) async-start(), calls=%async_computation.1 | async-start | bytes 8912896 | tf_op jit(solution)/shard_map/psum | solution.py:31
  11.0 21.6 %copy-start.1 = (bf16[3840,512]{1,0:T(8,128)(2,1)S(1)}, bf16[3840,512]{1,0:T(8,128)(2,1)}, u32[]{:S(2)}) copy-start(bf16[3840,512]{1,0:T(8,128)(2,1)} %param.7) | copy-start | bytes 11796484
  26.5 6.1 copy-start
  44.0 213.5 %all-reduce.6.cloned.1.call-start = ((), (), s32[]{:S(2)}) async-start(), calls=%async_computation.2 | async-start | bytes 2097152 | tf_op jit(solution)/shard_map/psum | solution.py:33
  222.0 270.7 %reduce-scatter.2.cloned.1.call-start = ((), (), s32[]{:S(2)}) async-start(), calls=%async_computation.3 | async-start | bytes 9830400 | tf_op jit(solution)/shard_map/reduce_scatter | solution.py:36
  422.5 148.9 %all-gather.5.cloned.1.call-start = ((), (), s32[]{:S(2)}) async-start(), calls=%async_computation.5 | async-start | bytes 4915200 | tf_op jit(solution)/shard_map/all_gather | solution.py:50
  537.5 68.3 %all-gather.3.cloned.1.call-start = ((), (), s32[]{:S(2)}) async-start(), calls=%async_computation.4 | async-start | bytes 4915200 | tf_op jit(solution)/shard_map/all_gather | solution.py:49
Sparse Core Ops, SparseCore 0:
  44.1 165.7 all-reduce.3
  222.1 35.2 all-reduce.5
  422.6 69.9 reduce-scatter.1
  537.7 33.6 all-gather.4
  572.8 32.9 all-gather.2
where the time goes:
time: 643 us; the launch traced here: 635 us
  waiting for transfers between devices  325 us (51%)
  other arithmetic  143 us (22%)
  matrix products  85.4 us (13%)
  blocking collectives  39.3 us (6%)
  local copies, waits for them, and re-layouts  24.7 us (4%)
  between operations  18.1 us (3%)
    psum x1, waiting for transfers between devices, on_device(): left_part = lax.psum(partial_left, 'col')  166 us
    another operation x14, other arithmetic, tri_inverse(): lower_factor = jnp.linalg.cholesky(gram_matrix)  79 us
    reduce_scatter x1, waiting for transfers between devices, on_device(): lax.psum_scatter(lax.dot_general(buffer, ortho, (((0,), (0,)), ((), ())),...  70.1 us
    another operation x3, other arithmetic, tri_inverse(): return jax.scipy.linalg.solve_triangular(lower_factor, ident, lower=True)  40.3 us
    psum x1, blocking collectives, on_device(): squares = lax.psum(jnp.sum(right_part * right_part, axis=0), ('row', 'col'))  39.3 us
    psum x1, waiting for transfers between devices, on_device(): gram_matrix = lax.psum(gram_local, 'row')  34.3 us
    all_gather x1, waiting for transfers between devices, on_device(): lax.all_gather(basis_piece, 'row', axis=0, tiled=True)  33.3 us
    all_gather x1, waiting for transfers between devices, on_device(): lax.all_gather(right_piece, 'row', axis=0, tiled=True)  20.5 us
  transfers between devices with their start and end apart: 5, of which 5 were waited for; matrix products, arithmetic and copies ran while one was open for 2% of the time, Pallas kernels for 0%

commit v1 on v0

--- a/solution.py
+++ b/solution.py
@@ -10,6 +10,14 @@
 BLOCK = 128
 EPS = 1e-06
 ERR = 0.05
+
+
+def doubling_sum(x, name):
+    size, acc = (lax.axis_size(name), x)
+    for far in [1 << k for k in range(size.bit_length() - 1)]:
+        swap = [(i, i ^ far) for i in range(size)]
+        acc = acc + lax.ppermute(acc, name, swap)
+    return acc
 
 
 def tri_inverse(gram_matrix):
@@ -30,7 +38,7 @@
     partial_left = jnp.dot(buffer, prev_basis, preferred_element_type=jnp.float32)
     left_part = lax.psum(partial_left, "col")
     gram_local = jnp.dot(left_part.T, left_part, precision=lax.Precision.HIGHEST)
-    gram_matrix = lax.psum(gram_local, "row")
+    gram_matrix = doubling_sum(gram_local, "row")
     inverse = tri_inverse(gram_matrix)
     ortho = jnp.dot(left_part, inverse.T, precision=lax.Precision.HIGHEST).astype(jnp.bfloat16)
     right_part = lax.psum_scatter(

time: 643 us -> 637 us (level)
  waiting for transfers between devices: 325 us -> 315 us
    psum x1 -> x0, waiting for transfers between devices: 34.3 us -> none  [on_device(): gram_matrix = lax.psum(gram_local, 'row')]
    ppermute x0 -> x2, waiting for transfers between devices: none -> 26.3 us  [doubling_sum(): acc = acc + lax.ppermute(acc, name, swap)]
  transfers between devices with their start and end apart: 5 -> 6, of which waited for: 5 -> 6; matrix products, arithmetic and copies ran while one was open for 2% -> 2% of each run, Pallas kernels for 0% -> 0%
where the time goes in v1:
time: 637 us; the launch traced here: 629 us
  waiting for transfers between devices  315 us (49%)
  other arithmetic  142 us (22%)
  matrix products  87.6 us (14%)
  blocking collectives  39.3 us (6%)
  local copies, waits for them, and re-layouts  24.5 us (4%)
  between operations  18.1 us (3%)
    psum x1, waiting for transfers between devices, on_device(): left_part = lax.psum(partial_left, 'col')  166 us
    another operation x14, other arithmetic, tri_inverse(): lower_factor = jnp.linalg.cholesky(gram_matrix)  79 us
    reduce_scatter x1, waiting for transfers between devices, on_device(): lax.psum_scatter(lax.dot_general(buffer, ortho, (((0,), (0,)), ((), ())),...  68.6 us
    another operation x3, other arithmetic, tri_inverse(): return jax.scipy.linalg.solve_triangular(lower_factor, ident, lower=True)  40.2 us
    psum x1, blocking collectives, on_device(): squares = lax.psum(jnp.sum(right_part * right_part, axis=0), ('row', 'col'))  39.3 us
    all_gather x1, waiting for transfers between devices, on_device(): lax.all_gather(basis_piece, 'row', axis=0, tiled=True)  33.3 us
    ppermute x2, waiting for transfers between devices, doubling_sum(): acc = acc + lax.ppermute(acc, name, swap)  26.3 us
    all_gather x1, waiting for transfers between devices, on_device(): lax.all_gather(right_piece, 'row', axis=0, tiled=True)  20.5 us
  transfers between devices with their start and end apart: 6, of which 6 were waited for; matrix products, arithmetic and copies ran while one was open for 2% of the time, Pallas kernels for 0%

profile of v1, /device:TPU:0, one launch (start us, length us, event | category | flops | bytes accessed | tf_op | source)
XLA Modules:
  0.0 628.7 jit_solution(7521490467311702667)
XLA Ops:
  11.0 15.4 %and_select_fusion = bf16[2176,3840]{1,0:T(8,128)(2,1)S(1)} fusion(bf16[2176,3840]{1,0:T(8,128)(2,1)} %param.6, bf16[2176,3840]{1,0:T(8,128)(2,1)} %param.5, pred[3840]{0:T(1024)(128)(4,1)S(1)} %iota_compare_fusion.4, pred[2176]{0:T(1024)(128)(4,1)S(1)} %iota_compare_fusion.5), kind=kLoop, calls=%fused_computation.5 | loop fusion | flops 50135040 | bytes 50141056 | tf_op jit(solution)/shard_map/jit(_where)/select_n | solution.py:36
  26.5 6.1 copy-done
  32.6 11.3 %fusion = f32[2176,512]{1,0:T(8,128)} fusion(bf16[2176,3840]{1,0:T(8,128)(2,1)S(1)} %and_select_fusion, bf16[3840,512]{1,0:T(8,128)(2,1)S(1)} %copy-done.2, pred[3840]{0:T(1024)(128)(4,1)S(1)} %iota_compare_fusion.4), kind=kOutput, calls=%fused_computation.7 | convolution fusion | flops 8558346240 | bytes 25104128 | tf_op jit(solution)/shard_map/dot_general | solution.py:38
  44.0 165.8 %all-reduce.3.cloned.1.call-done = f32[2176,512]{1,0:T(8,128)} async-done(((f32[2176,512]{1,0:T(8,128)}), f32[2176,512]{1,0:T(8,128)}) %all-reduce.3.cloned.1.call-update) | async-done | bytes 4456464 | tf_op jit(solution)/shard_map/psum | solution.py:39
  209.9 11.5 %fusion.50 = f32[512,512]{0,1:T(8,128)S(1)} fusion(f32[2176,512]{1,0:T(8,128)} %all-reduce.3.cloned.1.call-done), kind=kOutput, calls=%fused_computation.94 | convolution fusion | flops 6845104128 | bytes 5505024 | tf_op jit(solution)/shard_map/dot_general | solution.py:40
  226.1 23.6 %collective-permute-done.1 = f32[512,512]{0,1:T(8,128)} collective-permute-done((f32[512,512]{0,1:T(8,128)S(1)}, f32[512,512]{0,1:T(8,128)}, u32[]{:S(2)}, u32[]{:S(2)}) %collective-permute-start.1) | collective-permute-done | bytes 1048608 | tf_op jit(solution)/shard_map/ppermute | solution.py:19
  252.7 11.7 %cholesky.104 = f32[128,128]{1,0:T(8,128)S(1)} custom-call(f32[128,128]{1,0:T(8,128)S(1)} %cholesky.266), custom_call_target="Cholesky" | custom-call | tf_op jit(solution)/shard_map/jit(cholesky)/cholesky | solution.py:24
  264.4 9.8 %custom-call.31 = f32[1,128,128]{1,2,0:T(8,128)S(1)} custom-call(f32[1,128,128]{2,1,0:T(8,128)S(1)} %get-tuple-element.32), custom_call_target="InvertDiagBlocksLowerTriangular" | custom-call | tf_op jit(solution)/shard_map/jit(cholesky)/cholesky | solution.py:24
  276.9 11.7 %cholesky.217 = f32[128,128]{1,0:T(8,128)S(1)} custom-call(f32[128,128]{1,0:T(8,128)S(1)} %cholesky.270), custom_call_target="Cholesky" | custom-call | tf_op jit(solution)/shard_map/jit(cholesky)/cholesky | solution.py:24
  288.6 10.0 %custom-call.32 = f32[1,128,128]{1,2,0:T(8,128)S(1)} custom-call(f32[1,128,128]{2,1,0:T(8,128)S(1)} %get-tuple-element.29), custom_call_target="InvertDiagBlocksLowerTriangular" | custom-call | tf_op jit(solution)/shard_map/jit(cholesky)/cholesky | solution.py:24
  300.2 11.7 %cholesky.238 = f32[128,128]{1,0:T(8,128)S(1)} custom-call(f32[128,128]{1,0:T(8,128)S(1)} %cholesky.275), custom_call_target="Cholesky" | custom-call | tf_op jit(solution)/shard_map/jit(cholesky)/cholesky | solution.py:24
  312.6 9.8 %custom-call.33 = f32[1,128,128]{1,2,0:T(8,128)S(1)} custom-call(f32[1,128,128]{2,1,0:T(8,128)S(1)} %get-tuple-element.26), custom_call_target="InvertDiagBlocksLowerTriangular" | custom-call | tf_op jit(solution)/shard_map/jit(cholesky)/cholesky | solution.py:24
  323.9 12.1 %cholesky.255 = f32[128,128]{1,0:T(8,128)S(1)} custom-call(f32[128,128]{1,0:T(8,128)S(1)} %slice_subtract_fusion.2), custom_call_target="Cholesky" | custom-call | tf_op jit(solution)/shard_map/jit(cholesky)/cholesky | solution.py:24
  340.1 10.2 %while.1 = (s32[]{:T(128)}, f32[512,512]{1,0:T(8,128)S(1)}, s32[4,2]{0,1:T(2,128)S(1)}, f32[4,128,128]{2,1,0:T(8,128)}, s32[]{:T(128)}) while((s32[]{:T(128)}, f32[512,512]{1,0:T(8,128)S(1)}, s32[4,2]{0,1:T(2,128)S(1)}, f32[4,128,128]{2,1,0:T(8,128)}, s32[]{:T(128)}) %tuple.32), condition=%wide.while_cond, body=%wide.while_body.sunk | while | flops 2 | bytes 132205 | solution.py:26
  350.2 40.1 %custom-call.34 = f32[4,128,128]{1,2,0:T(8,128)S(1)} custom-call(f32[4,128,128]{2,1,0:T(8,128)} %get-tuple-element.10), custom_call_target="InvertDiagBlocksLowerTriangular" | custom-call | tf_op jit(solution)/shard_map/jit(_solve_triangular)/triangular_solve | solution.py:26
  393.4 9.0 %convolution_convert_fusion = bf16[2176,512]{1,0:T(8,128)(2,1)S(1)} fusion(f32[2176,512]{1,0:T(8,128)} %all-reduce.3.cloned.1.call-done, f32[128,512]{1,0:T(8,128)S(1)} %fusion.33, f32[128,512]{1,0:T(8,128)S(1)} %fusion.34, f32[128,512]{1,0:T(8,128)S(1)} %fusion.36, f32[128,512]{1,0:T(8,128)S(1)} %fusion.23), kind=kOutput, calls=%fused_computation.6 | convolution fusion | flops 6847004672 | bytes 7733248 | tf_op jit(solution)/shard_map/dot_general | solution.py:43
  402.4 15.1 %fusion.51 = f32[3840,512]{1,0:T(8,128)} fusion(bf16[2176,3840]{1,0:T(8,128)(2,1)} %copy-done, bf16[2176,512]{1,0:T(8,128)(2,1)S(1)} %convolution_convert_fusion), kind=kOutput, calls=%fused_computation.95 | convolution fusion | flops 8556380160 | bytes 26804224 | tf_op jit(solution)/shard_map/dot_general | solution.py:45
  417.6 68.6 %reduce-scatter.2.cloned.1.call-done = f32[960,512]{1,0:T(8,128)} async-done(((f32[3840,512]{1,0:T(8,128)}), f32[960,512]{1,0:T(8,128)}) %reduce-scatter.2.cloned.1.call-update) | async-done | bytes 1966096 | tf_op jit(solution)/shard_map/reduce_scatter | solution.py:44
  487.9 39.3 %psum.15 = f32[512]{0:T(512)S(1)} all-reduce(f32[512]{0:T(512)S(1)} %multiply_reduce_fusion), channel_id=1, replica_groups=mesh['row'=4,'col'=8] {'row','col'}, use_global_device_ids=true, to_apply=%region_11.12 | all-reduce | flops 512 | bytes 4096 | tf_op jit(solution)/shard_map/psum | solution.py:52
  531.7 33.3 %all-gather.5.cloned.1.call-done = bf16[3840,512]{1,0:T(8,128)(2,1)} async-done(((bf16[960,512]{1,0:T(8,128)(2,1)}), bf16[3840,512]{1,0:T(8,128)(2,1)}) %all-gather.5.cloned.1.call-update) | async-done | bytes 3932176 | tf_op jit(solution)/shard_map/all_gather | solution.py:58
  565.0 13.9 %multiply_convert_fusion = bf16[2176,3840]{1,0:T(8,128)(2,1)} fusion(bf16[2176,512]{1,0:T(8,128)(2,1)S(1)} %convolution_convert_fusion, bf16[3840,512]{1,0:T(8,128)(2,1)} %all-gather.5.cloned.1.call-done), kind=kOutput, calls=%fused_computation.2 | convolution fusion | flops 8573091840 | bytes 22872064 | tf_op jit(solution)/shard_map/dot_general | solution.py:64
  578.9 20.5 %all-gather.3.cloned.1.call-done = bf16[3840,512]{1,0:T(8,128)(2,1)} async-done(((bf16[960,512]{1,0:T(8,128)(2,1)}), bf16[3840,512]{1,0:T(8,128)(2,1)}) %all-gather.3.cloned.1.call-update) | async-done | bytes 3932176 | tf_op jit(solution)/shard_map/all_gather | solution.py:57
  599.4 18.3 %subtract_convert_fusion = bf16[2176,3840]{1,0:T(8,128)(2,1)} fusion(bf16[2176,3840]{1,0:T(8,128)(2,1)} %copy-done, bf16[2176,512]{1,0:T(8,128)(2,1)S(1)} %convolution_convert_fusion, bf16[3840,512]{1,0:T(8,128)(2,1)} %all-gather.3.cloned.1.call-done), kind=kOutput, calls=%fused_computation.3 | convolution fusion | flops 8589803520 | bytes 39583744 | tf_op jit(solution)/shard_map/dot_general | solution.py:60
  617.7 4.3 copy.30
  (69 shorter events, 37.5 us)
Async XLA Ops:
  7.2 202.7 %all-reduce.3.cloned.1.call-start = ((), (), s32[]{:S(2)}) async-start(), calls=%async_computation.1 | async-start | bytes 8912896 | tf_op jit(solution)/shard_map/psum | solution.py:39
  11.0 21.6 %copy-start.2 = (bf16[3840,512]{1,0:T(8,128)(2,1)S(1)}, bf16[3840,512]{1,0:T(8,128)(2,1)}, u32[]{:S(2)}) copy-start(bf16[3840,512]{1,0:T(8,128)(2,1)} %param.7) | copy-start | bytes 11796484
  26.5 6.1 copy-start
  44.0 442.2 %reduce-scatter.2.cloned.1.call-start = ((), (), s32[]{:S(2)}) async-start(), calls=%async_computation.2 | async-start | bytes 9830400 | tf_op jit(solution)/shard_map/reduce_scatter | solution.py:44
  221.4 2.7 collective-permute-start
  224.3 25.4 %collective-permute-start.1 = (f32[512,512]{0,1:T(8,128)S(1)}, f32[512,512]{0,1:T(8,128)}, u32[]{:S(2)}, u32[]{:S(2)}) collective-permute-start(f32[512,512]{0,1:T(8,128)S(1)} %add.71), channel_id=1, source_target_pairs={{0,16},{8,24},{16,0},{24,8},{1,17},{9,25},{17,1},{25,9},{2,18},{10... | collective-permute-start | bytes 3145736 | tf_op jit(solution)/shard_map/ppermute | solution.py:19
  251.7 1.0 copy-start.1
  417.6 147.4 %all-gather.5.cloned.1.call-start = ((), (), s32[]{:S(2)}) async-start(), calls=%async_computation.4 | async-start | bytes 4915200 | tf_op jit(solution)/shard_map/all_gather | solution.py:58
  531.1 68.3 %all-gather.3.cloned.1.call-start = ((), (), s32[]{:S(2)}) async-start(), calls=%async_computation.3 | async-start | bytes 4915200 | tf_op jit(solution)/shard_map/all_gather | solution.py:57
Sparse Core Ops, SparseCore 0:
  44.1 165.7 all-reduce.2
  417.7 68.4 reduce-scatter.1
  531.2 33.7 all-gather.4
  566.4 32.9 all-gather.2
